TPU v7x, 32 devices: a whole 2x2x4 slice. The times are simulated.
32 devices in a mesh: fsdp: 16 (over z, y, x), tp: 2 (over core).
Axes of the slice: x: 2, y: 2, z: 4, core: 2. Of those that a mesh axis runs over, the one named last changes fastest.
Arguments:
- inputs: bfloat16 [4096, 4096], P('fsdp'), may hold values from -6 to 6
- value_grad: bfloat16 [4096, 1024], P('fsdp', 'tp'), may hold values from -24 to 24
- value_weight: bfloat16 [4096, 1024], P('tp', 'fsdp'), may hold values from -0.09375 to 0.09375
- counts: int32 [16, 4], P('fsdp'), may hold values from 1 to 232, as said below
- offsets: int32 [16, 4], P('fsdp'), may hold values from 0 to 248, as said below
Outputs:
- input_grad: bfloat16 [4096, 4096], P('fsdp', 'tp')
- weight_grad: float32 [4096, 1024], P('fsdp', 'tp')
Inputs may be any that keep to these rules, and one draw needn't show every extreme that they name: `offsets`: on each index of fsdp the 4 samples lie in order; each starts at a multiple of 8, at or after the 8-row-aligned end of the previous one, and all lie within the 256 rows; on some index the aligned blocks of its samples fill all 256 rows. `counts`: how many rows the samples of a row group fill varies widely between indices of fsdp.
All inputs are finite; a program needn't handle non-finite values.
Results may differ from a plain program's by a relative error of at most 0.0046.
Values may be sent and summed in bfloat16 or wider, within the bound.
A program may use at most 64 MiB of HBM per device.

v0:
```python
import math
import jax
import jax.numpy as jnp
from jax import lax
from jax.sharding import PartitionSpec as P


def local(inputs, value_grad, value_weight, counts, offsets):
    tok_rows = inputs.shape[0]
    row_block = min(128, tok_rows)
    positions = jnp.arange(tok_rows, dtype=jnp.int32)[:, None]
    starts = offsets[0][None, :]
    lengths = counts[0][None, :]
    inside = (positions >= starts) & (positions < starts + lengths)
    inverse_root = lax.rsqrt(lengths.astype(jnp.float32))
    row_factor = jnp.sum(jnp.where(inside, inverse_root, jnp.zeros_like(inverse_root)), axis=1)
    scaled = (value_grad.astype(jnp.float32) * row_factor[:, None]).astype(jnp.bfloat16)
    live_end = jnp.max(offsets[0] + counts[0])
    live_blocks = (live_end + row_block - 1) // row_block
    scaled_all = lax.all_gather(scaled, "tp", axis=1, tiled=True)
    empty_inputs = jnp.zeros((tok_rows, value_weight.shape[0]), jnp.float32)
    piece = lax.all_gather(value_weight, "fsdp", axis=1, tiled=True)

    def add_add_block(block_index, partial_value):
        lower = lax.dynamic_slice_in_dim(scaled_all, block_index * row_block, row_block, 0)
        before = lax.dynamic_slice_in_dim(partial_value, block_index * row_block, row_block, 0)
        product = lax.dot_general(
            lower, piece, (((1,), (1,)), ((), ())), preferred_element_type=jnp.float32
        )
        return lax.dynamic_update_slice_in_dim(
            partial_value, before + product, block_index * row_block, 0
        )

    result = lax.fori_loop(0, live_blocks, add_add_block, empty_inputs)
    input_grad = result.astype(jnp.bfloat16)
    normalizer = 1.0 / math.sqrt(counts.shape[1] * lax.axis_size("fsdp"))
    empty = jnp.zeros((inputs.shape[1], scaled.shape[1]), jnp.float32)

    def weight_add_block(block_index, partial_value):
        feature_rows = lax.dynamic_slice_in_dim(inputs, block_index * row_block, row_block, 0)
        grad_rows = lax.dynamic_slice_in_dim(scaled, block_index * row_block, row_block, 0)
        return partial_value + lax.dot_general(
            feature_rows, grad_rows, (((0,), (0,)), ((), ())), preferred_element_type=jnp.float32
        )

    result = lax.fori_loop(0, live_blocks, weight_add_block, empty)
    summed = lax.psum_scatter(result, "fsdp", scatter_dimension=0, tiled=True)
    return (input_grad, summed * normalizer)


def solution(mesh):
    in_specs = (P("fsdp", None), P("fsdp", "tp"), P("tp", "fsdp"), P("fsdp", None), P("fsdp", None))
    out_specs = (P("fsdp", "tp"), P("fsdp", "tp"))
    return jax.shard_map(local, mesh=mesh, in_specs=in_specs, out_specs=out_specs, check_vma=False)
```

profile of v0, /device:TPU:10, one launch (start us, length us, event | category | flops | bytes accessed | tf_op | source)
XLA Modules:
  0.0 278.1 jit_solution(10683928178615963049)
XLA Ops:
  7.2 0.0 all-gather.2.cloned.1.call-start
  7.2 0.7 all-gather.2.cloned.1.call-update
  7.9 0.0 reduce-scatter.2.cloned.1.call-start
  7.9 1.3 fusion.7
  9.9 0.7 rsqrt_bitcast_fusion
  10.6 0.7 add_bitcast_fusion
  11.3 0.7 select_reduce_fusion
  12.0 1.1 multiply_convert_fusion
  13.1 0.0 copy-start
  13.1 4.3 %broadcast_in_dim.30 = f32[4096,512]{1,0:T(8,128)} broadcast(f32[]{:T(128)} %constant.38.clone.1), dimensions={} | broadcast | bytes 8388612 | tf_op jit(solution)/shard_map/broadcast_in_dim | solution.py:37
  17.4 0.0 copy-done
  17.4 8.0 %while.21 = (s32[]{:T(128)}, f32[4096,512]{1,0:T(8,128)}, s32[]{:T(128)}, bf16[256,4096]{1,0:T(8,128)(2,1)S(1)}, bf16[256,512]{1,0:T(8,128)(2,1)S(1)}, /*index=5*/s32[]{:T(128)}, s32[]{:T(128)}, s32[]{:T(128)}, s32[]{:T(128)}) while((s32[]{:T(128)}, f32[4096,512]{1,0:T(8,128)}, s32[]{:T(128)}, bf16[256,4096]{1,0:T(8,128)(2,1)S(1)}, ...), condition=%wide.region_5.6_spmd, body=%wide.region_4.5_spmd.sunk | while | flops 538968064 | bytes 17958028 | solution.py:46
  17.4 8.0 %convolution_add_fusion.3 = f32[4096,512]{1,0:T(8,128)} fusion(f32[4096,512]{1,0:T(8,128)} %get-tuple-element.191, bf16[256,4096]{1,0:T(8,128)(2,1)S(1)} %get-tuple-element.202, s32[]{:T(128)S(6)} %select_n.24, bf16[256,512]{1,0:T(8,128)(2,1)S(1)} %get-tuple-element.203), kind=kOutput, calls=%fused_computation.4.clone.1 | convolution fusion | flops 538968064 | bytes 17957888 | tf_op jit(solution)/shard_map/while/body/dot_general | solution.py:42
  25.4 0.0 reduce-scatter.2.cloned.1.call-update
  25.4 2.2 all_gather.6
  27.6 59.9 %all-gather.2.cloned.1.call-done = bf16[2048,1024]{0,1:T(8,128)(2,1)} async-done(((bf16[2048,64]{0,1:T(8,128)(2,1)}), bf16[2048,1024]{0,1:T(8,128)(2,1)}) %all-gather.2.cloned.1.call-update) | async-done | bytes 4194320 | tf_op jit(solution)/shard_map/all_gather | solution.py:22
  87.5 6.4 %copy.9 = bf16[2048,1024]{1,0:T(8,128)(2,1)} copy(bf16[2048,1024]{0,1:T(8,128)(2,1)} %all-gather.2.cloned.1.call-done) | data formatting | bytes 8388608 | tf_op jit(solution)/shard_map/while | solution.py:34
  93.9 0.2 broadcast_in_dim.26
  94.1 4.0 %while.20 = (s32[]{:T(128)}, f32[256,2048]{1,0:T(8,128)S(1)}, s32[]{:T(128)}, bf16[256,1024]{1,0:T(8,128)(2,1)S(1)}, bf16[2048,1024]{1,0:T(8,128)(2,1)}, /*index=5*/s32[]{:T(128)}, s32[]{:T(128)}, s32[]{:T(128)}, s32[]{:T(128)}) while((s32[]{:T(128)}, f32[256,2048]{1,0:T(8,128)S(1)}, s32[]{:T(128)}, bf16[256,1024]{1,0:T(8,128)(2,1)S(1)}, ...), condition=%wide.region_3.4_spmd, body=%wide.region_2.3_spmd.sunk | while | flops 537133056 | bytes 6554763 | solution.py:34
  94.2 4.0 %fusion.16 = f32[256,2048]{1,0:T(8,128)S(1)} fusion(f32[256,2048]{1,0:T(8,128)S(1)} %get-tuple-element.164, s32[]{:T(128)S(6)} %select_n.23, bf16[2048,1024]{1,0:T(8,128)(2,1)} %get-tuple-element.176, bf16[256,1024]{1,0:T(8,128)(2,1)S(1)} %get-tuple-element.175), kind=kOutput, calls=%fused_computation.1.clone.1 | convolution fusion | flops 537133056 | bytes 6554624 | tf_op jit(solution)/shard_map/while/body/dot_general | solution.py:27
  98.1 1.1 convert_element_type.15
  99.3 170.2 %reduce-scatter.2.cloned.1.call-done = f32[256,512]{1,0:T(8,128)} async-done(((f32[4096,512]{1,0:T(8,128)}), f32[256,512]{1,0:T(8,128)}) %reduce-scatter.2.cloned.1.call-update) | async-done | bytes 524304 | tf_op jit(solution)/shard_map/reduce_scatter | solution.py:47
  269.4 1.9 broadcast_multiply_fusion
Async XLA Ops:
  7.2 80.3 %all-gather.2.cloned.1.call-start = ((), (), s32[]{:S(2)}) async-start(), calls=%async_computation.1 | async-start | bytes 4456448 | tf_op jit(solution)/shard_map/all_gather | solution.py:22
  7.9 261.5 %reduce-scatter.2.cloned.1.call-start = ((), (), s32[]{:S(2)}) async-start(), calls=%async_computation.2 | async-start | bytes 8912896 | tf_op jit(solution)/shard_map/reduce_scatter | solution.py:47
  13.1 4.3 %copy-start = (bf16[256,4096]{1,0:T(8,128)(2,1)S(1)}, bf16[256,4096]{1,0:T(8,128)(2,1)}, u32[]{:S(2)}) copy-start(bf16[256,4096]{1,0:T(8,128)(2,1)} %param.9) | copy-start | bytes 6291460
Sparse Core Ops, SparseCore 0:
  10.7 76.6 all-gather.1
  89.8 179.6 reduce-scatter.1
where the time goes:
time: 279 us; the launch traced here: 278 us
  waiting for transfers between devices  231 us (83%)
  between operations  14.7 us (5%)
  matrix products  12 us (4%)
  local copies, waits for them, and re-layouts  10.9 us (4%)
  other arithmetic  7.43 us (3%)
    reduce_scatter x1, waiting for transfers between devices, local(): summed = lax.psum_scatter(result, 'fsdp', scatter_dimension=0, tiled=True)  170 us
    all_gather x1, waiting for transfers between devices, local(): piece = lax.all_gather(value_weight, 'fsdp', axis=1, tiled=True)  59.9 us
    dot_general x1, matrix products, weight_add_block(): lax.dot_general(feature_rows, grad_rows, (((0,), (0,)), ((), ())), prefer...  7.98 us
    while x1, local copies, waits for them, and re-layouts, local(): result = lax.fori_loop(0, live_blocks, add_add_block, empty_inputs)  6.42 us
  transfers between devices with their start and end apart: 2, of which 2 were waited for; matrix products, arithmetic and copies ran while one was open for 10% of the time, Pallas kernels for 0%

commit v1 on v0

--- a/solution.py
+++ b/solution.py
@@ -19,7 +19,7 @@
     live_blocks = (live_end + row_block - 1) // row_block
     scaled_all = lax.all_gather(scaled, "tp", axis=1, tiled=True)
     empty_inputs = jnp.zeros((tok_rows, value_weight.shape[0]), jnp.float32)
-    piece = lax.all_gather(value_weight, "fsdp", axis=1, tiled=True)
+    piece = jnp.concatenate(lax.all_gather(value_weight, "fsdp"), axis=1)
 
     def add_add_block(block_index, partial_value):
         lower = lax.dynamic_slice_in_dim(scaled_all, block_index * row_block, row_block, 0)

time: 279 us -> 279 us (level)
  local copies, waits for them, and re-layouts: 10.9 us -> 19.8 us
  waiting for transfers between devices: 231 us -> 223 us
    reduce_scatter x1, waiting for transfers between devices: 170 us -> 162 us  [local(): summed = lax.psum_scatter(result, 'fsdp', scatter_dimension=0, tiled=True)]
    unnamed x2 -> x3, local copies, waits for them, and re-layouts: 0.01 us -> 4.59 us
    reshape x0 -> x1, local copies, waits for them, and re-layouts: none -> 4.25 us  [local(): piece = jnp.concatenate(lax.all_gather(value_weight, 'fsdp'), axis=1)]
  transfers between devices with their start and end apart: 2 -> 2, of which waited for: 2 -> 2; matrix products, arithmetic and copies ran while one was open for 10% -> 13% of each run, Pallas kernels for 0% -> 0%
where the time goes in v1:
time: 279 us
  waiting for transfers between devices  223 us (80%)
  local copies, waits for them, and re-layouts  19.8 us (7%)
  between operations  14.7 us (5%)
  matrix products  11.7 us (4%)
  other arithmetic  7.43 us (3%)
    reduce_scatter x1, waiting for transfers between devices, local(): summed = lax.psum_scatter(result, 'fsdp', scatter_dimension=0, tiled=True)  162 us
    all_gather x1, waiting for transfers between devices, local(): piece = jnp.concatenate(lax.all_gather(value_weight, 'fsdp'), axis=1)  59.6 us
    dot_general x1, matrix products, weight_add_block(): lax.dot_general(feature_rows, grad_rows, (((0,), (0,)), ((), ())), prefer...  7.99 us
    while x1, local copies, waits for them, and re-layouts, local(): result = lax.fori_loop(0, live_blocks, add_add_block, empty_inputs)  6.42 us
  transfers between devices with their start and end apart: 2, of which 2 were waited for; matrix products, arithmetic and copies ran while one was open for 13% of the time, Pallas kernels for 0%

profile of v1, /device:TPU:10, one launch (start us, length us, event | category | flops | bytes accessed | tf_op | source)
XLA Modules:
  0.0 278.6 jit_solution(16639860792189114490)
XLA Ops:
  7.2 0.0 all-gather.3.cloned.1.call-start
  7.2 0.7 all-gather.3.cloned.1.call-update
  7.9 0.0 reduce-scatter.2.cloned.1.call-start
  7.9 1.3 fusion.7
  9.9 0.7 rsqrt_bitcast_fusion
  10.6 0.7 add_bitcast_fusion
  11.3 0.7 select_reduce_fusion
  12.0 1.1 multiply_convert_fusion
  13.1 0.0 copy-start
  13.1 4.3 %broadcast_in_dim.30 = f32[4096,512]{1,0:T(8,128)} broadcast(f32[]{:T(128)} %constant.38.clone.1), dimensions={} | broadcast | bytes 8388612 | tf_op jit(solution)/shard_map/broadcast_in_dim | solution.py:37
  17.4 0.0 copy-done
  17.4 8.0 %while.21 = (s32[]{:T(128)}, f32[4096,512]{1,0:T(8,128)}, s32[]{:T(128)}, bf16[256,4096]{1,0:T(8,128)(2,1)S(1)}, bf16[256,512]{1,0:T(8,128)(2,1)S(1)}, /*index=5*/s32[]{:T(128)}, s32[]{:T(128)}, s32[]{:T(128)}, s32[]{:T(128)}) while((s32[]{:T(128)}, f32[4096,512]{1,0:T(8,128)}, s32[]{:T(128)}, bf16[256,4096]{1,0:T(8,128)(2,1)S(1)}, ...), condition=%wide.region_5.6_spmd, body=%wide.region_4.5_spmd.sunk | while | flops 538968064 | bytes 17958028 | solution.py:46
  17.4 8.0 %convolution_add_fusion.3 = f32[4096,512]{1,0:T(8,128)} fusion(f32[4096,512]{1,0:T(8,128)} %get-tuple-element.196, bf16[256,4096]{1,0:T(8,128)(2,1)S(1)} %get-tuple-element.207, s32[]{:T(128)S(6)} %select_n.24, bf16[256,512]{1,0:T(8,128)(2,1)S(1)} %get-tuple-element.208), kind=kOutput, calls=%fused_computation.4.clone.1 | convolution fusion | flops 538968064 | bytes 17957888 | tf_op jit(solution)/shard_map/while/body/dot_general | solution.py:42
  25.4 0.0 reduce-scatter.2.cloned.1.call-update
  25.4 2.2 all_gather.9
  27.6 59.6 %all-gather.3.cloned.1.call-done = bf16[32768,64]{0,1:T(8,128)(2,1)} async-done(((bf16[2048,64]{0,1:T(8,128)(2,1)}), bf16[32768,64]{0,1:T(8,128)(2,1)}) %all-gather.3.cloned.1.call-update) | async-done | bytes 4194320 | tf_op jit(solution)/shard_map/all_gather | solution.py:22
  87.2 4.6 %copy.13 = bf16[8,8,16,2048]{3,2,1,0:T(8,128)(2,1)S(1)} copy(bf16[8,8,16,2048]{3,1,2,0:T(8,128)(2,1)} %bitcast.22) | data formatting | bytes 8388608
  91.8 4.3 %copy.11 = bf16[2048,16,64]{0,2,1:T(8,128)(2,1)} copy(bf16[2048,16,64]{0,1,2:T(8,128)(2,1)S(1)} %bitcast.20) | data formatting | bytes 8388608 | tf_op jit(solution)/shard_map/reshape | solution.py:22
  96.0 6.4 %copy.12 = bf16[2048,1024]{1,0:T(8,128)(2,1)} copy(bf16[2048,1024]{0,1:T(8,128)(2,1)} %bitcast.21) | data formatting | bytes 8388608 | tf_op jit(solution)/shard_map/while | solution.py:34
  102.5 0.2 broadcast_in_dim.26
  102.7 3.7 %while.20 = (s32[]{:T(128)}, f32[256,2048]{1,0:T(8,128)S(1)}, s32[]{:T(128)}, bf16[256,1024]{1,0:T(8,128)(2,1)S(1)}, bf16[2048,1024]{1,0:T(8,128)(2,1)}, /*index=5*/s32[]{:T(128)}, s32[]{:T(128)}, s32[]{:T(128)}, s32[]{:T(128)}) while((s32[]{:T(128)}, f32[256,2048]{1,0:T(8,128)S(1)}, s32[]{:T(128)}, bf16[256,1024]{1,0:T(8,128)(2,1)S(1)}, ...), condition=%wide.region_3.4_spmd, body=%wide.region_2.3_spmd.sunk | while | flops 537133056 | bytes 6554763 | solution.py:34
  102.7 3.7 %fusion.16 = f32[256,2048]{1,0:T(8,128)S(1)} fusion(f32[256,2048]{1,0:T(8,128)S(1)} %get-tuple-element.169, s32[]{:T(128)S(6)} %select_n.23, bf16[2048,1024]{1,0:T(8,128)(2,1)} %get-tuple-element.181, bf16[256,1024]{1,0:T(8,128)(2,1)S(1)} %get-tuple-element.180), kind=kOutput, calls=%fused_computation.1.clone.1 | convolution fusion | flops 537133056 | bytes 6554624 | tf_op jit(solution)/shard_map/while/body/dot_general | solution.py:27
  106.4 1.1 convert_element_type.15
  107.5 162.4 %reduce-scatter.2.cloned.1.call-done = f32[256,512]{1,0:T(8,128)} async-done(((f32[4096,512]{1,0:T(8,128)}), f32[256,512]{1,0:T(8,128)}) %reduce-scatter.2.cloned.1.call-update) | async-done | bytes 524304 | tf_op jit(solution)/shard_map/reduce_scatter | solution.py:47
  269.9 1.9 broadcast_multiply_fusion
Async XLA Ops:
  7.2 80.0 %all-gather.3.cloned.1.call-start = ((), (), s32[]{:S(2)}) async-start(), calls=%async_computation.2 | async-start | bytes 4456448 | tf_op jit(solution)/shard_map/all_gather | solution.py:22
  7.9 262.0 %reduce-scatter.2.cloned.1.call-start = ((), (), s32[]{:S(2)}) async-start(), calls=%async_computation.1 | async-start | bytes 8912896 | tf_op jit(solution)/shard_map/reduce_scatter | solution.py:47
  13.1 4.3 %copy-start = (bf16[256,4096]{1,0:T(8,128)(2,1)S(1)}, bf16[256,4096]{1,0:T(8,128)(2,1)}, u32[]{:S(2)}) copy-start(bf16[256,4096]{1,0:T(8,128)(2,1)} %param.9) | copy-start | bytes 6291460
Sparse Core Ops, SparseCore 0:
  10.7 76.4 all-gather.2
  89.5 180.3 reduce-scatter.1
